TPU v7x, 32 devices: a whole 2x2x4 slice. The times are simulated.
32 devices in a mesh: head: 4 (over y, core), seq: 8 (over z, x).
Axes of the slice: x: 2, y: 2, z: 4, core: 2. Of those that a mesh axis runs over, the one named last changes fastest.
Arguments:
- queries: bfloat16 [2, 4, 32, 128], P(None, None, ('head', 'seq')), may hold values from -16 to 16
- keys: bfloat16 [2, 4, 16384, 128], P(None, 'head', 'seq'), may hold values from -6 to 6
- values: bfloat16 [2, 4, 16384, 128], P(None, 'head', 'seq'), may hold values from -6 to 6
- indices: int32 [4, 8, 1024], P('head'), may hold values from 0 to 16383, as said below
- sizes: int32 [4, 8], P('head'), may hold values from 128 to 1024, as said below
- owners: int32 [4, 8], P('head'), may hold values from 0 to 7, as said below
Outputs:
- compact_values: bfloat16 [4, 24, 1024, 128], P('head', 'seq')
Inputs may be any that keep to these rules, and one draw needn't show every extreme that they name: `indices`: in each row of a head and fit, the 1024 positions are distinct and the first two are 0 and 1; only the first sizes[h,f] are used. `sizes`: multiples of 128; in each head one fit has 1024. `owners`: no index owns more than 3 fits of a head; in each head one index owns exactly 3.
All inputs are finite; a program needn't handle non-finite values.
Results may differ from a plain program's by a relative error of at most 0.008.
Values may be sent and summed in bfloat16 or wider, within the bound.
A program may use at most 128 MiB of HBM per device.

v0:
```python
import jax
import jax.numpy as jnp
from jax import lax
from jax.experimental import pallas as pl
from jax.experimental.pallas import tpu as pltpu
from jax.sharding import PartitionSpec as P

FITS_LAYER = 4
SLOTS = 3
RIDGE = 0.3
LANES = 128
FAR = -(2.0**100)
LOG2E = 1.4426950408889634
PAIR = 2

SUBLANES = 8
MESH = pl.DeviceIdType.MESH
NT = (((1,), (1,)), ((), ()))
TN = (((0,), (0,)), ((), ()))


def solve_rows(system, target):
    rows = system.shape[0]
    row = lax.broadcasted_iota(jnp.int32, (rows, 1), 0)
    if rows <= 64:
        for k in range(rows):
            inverse = 1.0 / system[k : k + 1, k : k + 1]
            pivot_s = system[k : k + 1, :] * inverse
            pivot_t = target[k : k + 1, :] * inverse
            column = jnp.where(row == k, system[:, k : k + 1] - 1.0, system[:, k : k + 1])
            system = system - column * pivot_s
            target = target - column * pivot_t
        return target
    lane = lax.broadcasted_iota(jnp.int32, (1, rows), 1)

    def step(k, state):
        system, target = state
        column = jnp.sum(jnp.where(lane == k, system, 0.0), axis=1, keepdims=True)
        here = row == k
        inverse = 1.0 / jnp.sum(jnp.where(here, column, 0.0), axis=0, keepdims=True)
        pivot_s = jnp.sum(jnp.where(here, system, 0.0), axis=0, keepdims=True) * inverse
        pivot_t = jnp.sum(jnp.where(here, target, 0.0), axis=0, keepdims=True) * inverse
        column = jnp.where(here, column - 1.0, column)
        return system - column * pivot_s, target - column * pivot_t

    return lax.fori_loop(0, rows, step, (system, target))[1]


def split_exponent(block, capacity):
    tail = block[:, capacity:].astype(jnp.float32)
    return block[:, :capacity].astype(jnp.float32), tail[:, 0:1] + tail[:, 64:65]


def joined_exponent(expo, top, lane):
    high = top.astype(jnp.bfloat16)
    low = (top - high.astype(jnp.float32)).astype(jnp.bfloat16)
    tail = jnp.where(lane < 64, high.astype(jnp.float32), low.astype(jnp.float32))
    return jnp.concatenate([expo.astype(jnp.bfloat16), tail.astype(jnp.bfloat16)], axis=1)


def enter(axes):
    barrier = pltpu.get_barrier_semaphore()
    total = 0
    for axis in axes:
        me, size = lax.axis_index(axis), lax.axis_size(axis)
        for step in range(1, size):
            pl.semaphore_signal(
                barrier, inc=1, device_id={axis: lax.rem(me + step, size)}, device_id_type=MESH
            )
        total += size - 1
    pl.semaphore_wait(barrier, total)


def send(source, target, send_sem, recv_sem, axis, peer):
    return pltpu.make_async_remote_copy(
        src_ref=source,
        dst_ref=target,
        send_sem=send_sem,
        recv_sem=recv_sem,
        device_id={axis: peer},
        device_id_type=MESH,
    )


def fit_kernel(
    sizes_ref, q_in, k_hbm, v_hbm, idx_ref, p_ref, x_ref,
    piece, column, table, k_ref, v_ref, s_ref, g_ref, part, part_in, chunk_mine, chunks, e_out, e_in, z_out, z_in,
    p_mine, p_all, x_mine, x_all,
    load, send_head, recv_head, send_seq, recv_seq, send_part, recv_part, send_chunk, recv_chunk, send_e, recv_e, send_z, recv_z,
    send_p, recv_p, send_f, recv_f, send_x, recv_x,
):
    layers, local_len, width = k_ref.shape
    fits, capacity = idx_ref.shape
    heads, my_head = lax.axis_size("head"), lax.axis_index("head")
    groups, me = lax.axis_size("seq"), lax.axis_index("seq")
    rows = groups * heads
    outer, inner = me // PAIR, lax.rem(me, PAIR)
    outers, half = groups // PAIR, fits // PAIR
    partner = outer * PAIR + 1 - inner
    fit_mine = jnp.minimum(me, fits - 1)
    chunk = layers * rows // groups
    start = me * local_len
    lane = lax.broadcasted_iota(jnp.int32, (rows, LANES), 1)
    exact = outers == half

    loads = [
        pltpu.make_async_copy(k_hbm, k_ref, load.at[0]),
        pltpu.make_async_copy(v_hbm, v_ref, load.at[1]),
    ]
    for copy in loads:
        copy.start()
    drawn_rows = q_in[...].astype(jnp.float32)
    for head in range(heads):
        for layer in range(layers):
            at = layer * heads + head
            piece[head, layer : layer + 1, :] = drawn_rows[at : at + 1]
        piece[head, layers:, :] = jnp.zeros((SUBLANES - layers, width), jnp.float32)
    enter(("head", "seq"))
    near = heads * SUBLANES
    column[pl.ds(pl.multiple_of(my_head * SUBLANES, SUBLANES), SUBLANES), :] = piece[my_head]
    first, second = [], []
    for step in range(1, heads):
        peer = lax.rem(my_head + step, heads)
        first.append(
            send(
                piece.at[peer],
                column.at[pl.ds(pl.multiple_of(my_head * SUBLANES, SUBLANES), SUBLANES), :],
                send_head.at[step], recv_head.at[step], "head", peer,
            )
        )
        first[-1].start()
    for copy in first:
        copy.wait_recv()
    for step in range(1, groups):
        peer = lax.rem(me + step, groups)
        second.append(
            send(
                column, table.at[pl.ds(pl.multiple_of(me * near, near), near), :],
                send_seq.at[step], recv_seq.at[step], "seq", peer,
            )
        )
        second[-1].start()
    table[pl.ds(pl.multiple_of(me * near, near), near), :] = column[...]
    for copy in second:
        copy.wait_recv()
    for copy in loads:
        copy.wait()

    for layer in range(layers):
        query_rows = table[pl.ds(layer, rows, stride=SUBLANES), :].astype(jnp.bfloat16)
        scores = lax.dot_general(
            query_rows, k_ref[layer], NT, preferred_element_type=jnp.float32
        ) * (width ** (-0.5) * LOG2E)
        s_ref[layer] = scores
        peak = jnp.max(scores, axis=1, keepdims=True)
        weights = jnp.exp2(scores - peak)
        total = jnp.sum(weights, axis=1, keepdims=True)
        numer = jnp.dot(
            weights.astype(jnp.bfloat16), v_ref[layer], preferred_element_type=jnp.float32
        )
        side = jnp.where(lane < 64, total, peak)
        for at in range(rows // chunk):
            slot = layer * (rows // chunk) + at
            part[slot, 0] = numer[at * chunk : (at + 1) * chunk]
            part[slot, 1] = side[at * chunk : (at + 1) * chunk]

    def produce(fit):
        layer = fit // FITS_LAYER
        size = sizes_ref[0, fit]

        def one_tile(tile, top):
            base = pl.multiple_of(tile * LANES, LANES)
            drawn = idx_ref[:, pl.ds(base, LANES)]
            mine = lax.broadcasted_iota(jnp.int32, (fits, LANES), 0) == fit
            offset = jnp.sum(jnp.where(mine, drawn, 0), axis=0, keepdims=True) - start
            column = base + lax.broadcasted_iota(jnp.int32, (1, LANES), 1)
            inside = (offset >= 0) & (offset < local_len) & (column < size)
            offset = jnp.broadcast_to(jnp.where(inside, offset, -1), (rows, LANES))
            high = offset >> 7
            low = offset & (LANES - 1)
            picked = jnp.full((rows, LANES), FAR, jnp.float32)
            for block in range(local_len // LANES):
                scored = s_ref[layer, :, block * LANES : (block + 1) * LANES]
                found = jnp.take_along_axis(scored, low, axis=1, mode="promise_in_bounds")
                picked = jnp.where(high == block, found, picked)
            g_ref[:, pl.ds(base, LANES)] = picked
            return jnp.maximum(top, jnp.max(picked, axis=1, keepdims=True))

        top = lax.fori_loop(
            0,
            capacity // LANES,
            one_tile,
            jnp.full((rows, 1), FAR, jnp.float32),
            unroll=4 if rows <= 64 else 1,
        )
        top = jnp.ceil(top)
        picked = g_ref[...]
        return jnp.where(picked > 0.5 * FAR, jnp.exp2(picked - top), 0.0), top

    parts = []
    for step in range(1, groups):
        peer = lax.rem(me + step, groups)
        parts.append(
            send(
                part.at[peer], part_in.at[step],
                send_part.at[step], recv_part.at[step], "seq", peer,
            )
        )
        parts[-1].start()
    part_in[0] = part[me]

    def column_of(j):
        return lax.rem(outer + 1 + j, outers) if exact else jnp.int32(j)

    across = []
    for j in range(half):
        expo, top = produce(column_of(j) * PAIR + 1 - inner)
        e_out[j] = joined_exponent(expo, top, lane)
        across.append(
            send(e_out.at[j], e_in.at[j], send_e.at[j], recv_e.at[j], "seq", partner)
        )
        if j > 0:
            across[j - 1].start()

    for copy in parts:
        copy.wait_recv()
    peak = part_in[0, 1][:, 64:65]
    for step in range(1, groups):
        peak = jnp.maximum(peak, part_in[step, 1][:, 64:65])
    numer, total = 0.0, 0.0
    for step in range(groups):
        factor = jnp.exp2(part_in[step, 1][:, 64:65] - peak)
        numer = numer + part_in[step, 0] * factor
        total = total + part_in[step, 1][:, 0:1] * factor
    merged = numer / total
    chunk_mine[...] = merged
    chunks[me] = merged
    across[half - 1].start()

    down, spread = [], []
    for j in range(half):
        dest = column_of(j)
        expo, top = produce(dest * PAIR + inner)
        if j == 0:
            for step in range(1, groups):
                peer = lax.rem(me + step, groups)
                spread.append(
                    send(
                        chunk_mine, chunks.at[me],
                        send_chunk.at[step], recv_chunk.at[step], "seq", peer,
                    )
                )
                spread[-1].start()
        across[j].wait_recv()
        other, other_top = split_exponent(e_in[j], capacity)
        both = jnp.maximum(top, other_top)
        expo = expo * jnp.exp2(top - both) + other * jnp.exp2(other_top - both)
        block = joined_exponent(expo, both, lane)
        copy = send(
            z_out.at[j], z_in.at[outer], send_z.at[j], recv_z.at[outer],
            "seq", dest * PAIR + inner,
        )
        down.append((dest, copy))
        if exact:
            if j == half - 1:
                z_in[outer] = block
            else:
                z_out[j] = block
                copy.start()
        else:
            z_out[j] = block
            pl.when(dest != outer)(copy.start)

            @pl.when(dest == outer)
            def _():
                z_in[outer] = block

    def only(condition, act):
        if exact:
            act()
        else:
            pl.when(condition)(act)

    def source_z(step):
        source = lax.rem(outer + step, outers)
        return source, send(
            z_out.at[0], z_in.at[source], send_z.at[0], recv_z.at[source], "seq", partner
        )

    def gave_p(step, target):
        return send(
            p_mine, p_all.at[fit_mine], send_p.at[step], recv_p.at[outer],
            "seq", target * PAIR + inner,
        )

    def came_p(source):
        fit = jnp.minimum(source, half - 1) * PAIR + inner
        arrival = send(
            p_mine, p_all.at[fit], send_p.at[0], recv_p.at[source], "seq", partner
        )
        onward = send(
            p_all.at[fit], p_all.at[fit], send_f.at[source], recv_f.at[source], "seq", partner
        )
        return arrival, onward

    def back_p(source):
        fit = jnp.minimum(source, half - 1) * PAIR + 1 - inner
        return send(
            p_mine, p_all.at[fit], send_f.at[source], recv_f.at[source], "seq", partner
        )

    gifts = [gave_p(step, lax.rem(outer + step, outers)) for step in range(1, outers)]
    own_onward = send(
        p_mine, p_all.at[fit_mine], send_f.at[outer], recv_f.at[outer], "seq", partner
    )
    results = [
        send(
            x_mine, x_all.at[fit_mine], send_x.at[step], recv_x.at[step],
            "seq", lax.rem(me + step, groups),
        )
        for step in range(1, groups)
    ]

    def relay():
        for step in range(1, outers):
            source = lax.rem(outer + outers - step, outers)
            arrival, onward = came_p(source)

            def pass_on():
                arrival.wait_recv()
                onward.start()

            only(source < half, pass_on)

    for copy in spread:
        copy.wait_recv()

    def work():
        for step in range(1, outers):
            source_z(step)[1].wait_recv()
        blocks = [split_exponent(z_in[source], capacity) for source in range(outers)]
        top = blocks[0][1]
        for _, other in blocks[1:]:
            top = jnp.maximum(top, other)
        probs = 0.0
        for expo, other in blocks:
            probs = probs + expo * jnp.exp2(other - top)
        probs = (probs / jnp.sum(probs, axis=1, keepdims=True)).astype(jnp.bfloat16)
        p_mine[...] = probs
        p_all[fit_mine] = probs
        gram = lax.dot_general(probs, probs, NT, preferred_element_type=jnp.float32)
        for copy in gifts:
            copy.start()
        own_onward.start()
        diagonal = lax.broadcasted_iota(jnp.int32, (rows, rows), 0) == lax.broadcasted_iota(
            jnp.int32, (rows, rows), 1
        )
        trace = jnp.sum(jnp.where(diagonal, gram, 0.0))
        ridge = RIDGE * trace / sizes_ref[0, fit_mine].astype(jnp.float32)
        span = rows // chunk
        base = (fit_mine // FITS_LAYER) * span
        target = jnp.concatenate([chunks[base + at] for at in range(span)], axis=0)
        target = target.astype(jnp.bfloat16).astype(jnp.float32)
        solved = solve_rows(jnp.where(diagonal, gram + ridge, gram), target)
        x_mine[...] = solved
        x_all[fit_mine] = solved
        for copy in results:
            copy.start()

    only(outer < half, work)
    relay()
    for copy in first + second + parts + spread + across:
        copy.wait_send()
    for j in range(half):
        dest, copy = down[j]
        if exact:
            if j < half - 1:
                copy.wait_send()
        else:
            pl.when(dest != outer)(copy.wait_send)
    for step in range(1, outers):
        source = lax.rem(outer + outers - step, outers)
        only(outer < half, gifts[step - 1].wait_send)
        only(source < half, came_p(source)[1].wait_send)
    only(outer < half, own_onward.wait_send)
    for source in range(half):
        back_p(source).wait_recv()
    for step in range(1, groups):
        source = lax.rem(me + groups - step, groups)
        only(source < fits, results[step - 1].wait_recv)
        only(outer < half, results[step - 1].wait_send)
    p_ref[...] = p_all[...]
    x_ref[...] = x_all[...]


def place_kernel(owners_ref, p_ref, x_ref, out_ref):
    me = lax.axis_index("seq")
    fits = p_ref.shape[0]
    count = jnp.int32(0)
    chosen = [jnp.int32(0)] * SLOTS
    for fit in range(fits):
        mine = owners_ref[0, fit] == me
        for slot in range(SLOTS):
            chosen[slot] = jnp.where(mine & (count == slot), fit, chosen[slot])
        count = count + mine.astype(jnp.int32)
    for slot in range(SLOTS):

        @pl.when(count > slot)
        def _():
            probs = p_ref[chosen[slot]]
            rows = x_ref[chosen[slot]]
            high = rows.astype(jnp.bfloat16)
            low = (rows - high.astype(jnp.float32)).astype(jnp.bfloat16)
            out_ref[0, slot] = lax.dot_general(
                jnp.concatenate([probs, probs], axis=0),
                jnp.concatenate([high, low], axis=0),
                TN,
                preferred_element_type=jnp.float32,
            ).astype(jnp.bfloat16)

        @pl.when(count <= slot)
        def _():
            out_ref[0, slot] = jnp.zeros(out_ref.shape[2:], jnp.bfloat16)


VMEM = pl.BlockSpec(memory_space=pltpu.VMEM)
ANY = pl.BlockSpec(memory_space=pl.ANY)
SMEM = pl.BlockSpec(memory_space=pltpu.SMEM)
PARAMS = dict(vmem_limit_bytes=60 * 1024 * 1024)


def on_device(queries, keys, values, indices, sizes, owners):
    layers, heads, count, width = queries.shape
    groups = lax.axis_size("seq")
    rows = groups * heads * count
    local_len = keys.shape[2]
    fits, capacity = indices.shape[1:]
    dma = pltpu.SemaphoreType.DMA
    outers, half = groups // PAIR, fits // PAIR
    chunk = layers * rows // groups
    packed = (rows, capacity + LANES)
    probs, solved = pl.pallas_call(
        fit_kernel,
        out_shape=(
            jax.ShapeDtypeStruct((fits, rows, capacity), jnp.bfloat16),
            jax.ShapeDtypeStruct((fits, rows, width), jnp.float32),
        ),
        in_specs=[SMEM, VMEM, ANY, ANY, VMEM],
        out_specs=(VMEM, VMEM),
        scratch_shapes=[
            pltpu.VMEM((heads, SUBLANES, width), jnp.float32),
            pltpu.VMEM((heads * SUBLANES, width), jnp.float32),
            pltpu.VMEM((rows * SUBLANES, width), jnp.float32),
            pltpu.VMEM((layers, local_len, width), jnp.bfloat16),
            pltpu.VMEM((layers, local_len, width), jnp.bfloat16),
            pltpu.VMEM((layers, rows, local_len), jnp.float32),
            pltpu.VMEM((rows, capacity), jnp.float32),
            pltpu.VMEM((groups, 2, chunk, width), jnp.float32),
            pltpu.VMEM((groups, 2, chunk, width), jnp.float32),
            pltpu.VMEM((chunk, width), jnp.float32),
            pltpu.VMEM((groups, chunk, width), jnp.float32),
            pltpu.VMEM((half,) + packed, jnp.bfloat16),
            pltpu.VMEM((half,) + packed, jnp.bfloat16),
            pltpu.VMEM((half,) + packed, jnp.bfloat16),
            pltpu.VMEM((outers,) + packed, jnp.bfloat16),
            pltpu.VMEM((rows, capacity), jnp.bfloat16),
            pltpu.VMEM((fits, rows, capacity), jnp.bfloat16),
            pltpu.VMEM((rows, width), jnp.float32),
            pltpu.VMEM((fits, rows, width), jnp.float32),
            dma((2,)),
            dma((heads,)),
            dma((heads,)),
            dma((groups,)),
            dma((groups,)),
            dma((groups,)),
            dma((groups,)),
            dma((groups,)),
            dma((groups,)),
            dma((half,)),
            dma((half,)),
            dma((half,)),
            dma((outers,)),
            dma((outers,)),
            dma((outers,)),
            dma((outers,)),
            dma((outers,)),
            dma((groups,)),
            dma((groups,)),
        ],
        compiler_params=pltpu.CompilerParams(collective_id=2, has_side_effects=True, **PARAMS),
    )(
        sizes,
        queries.reshape(layers * heads, width),
        keys[:, 0],
        values[:, 0],
        indices[0],
    )
    return pl.pallas_call(
        place_kernel,
        out_shape=jax.ShapeDtypeStruct((1, SLOTS, capacity, width), jnp.bfloat16),
        in_specs=[SMEM, VMEM, VMEM],
        out_specs=VMEM,
        compiler_params=pltpu.CompilerParams(**PARAMS),
    )(owners, probs, solved)


def solution(mesh):
    in_specs = (
        P(None, None, ("head", "seq"), None),
        P(None, "head", "seq", None),
        P(None, "head", "seq", None),
        P("head", None, None),
        P("head", None),
        P("head", None),
    )
    out_specs = P("head", "seq", None, None)
    return jax.shard_map(
        on_device, mesh=mesh, in_specs=in_specs, out_specs=out_specs, check_vma=False
    )
```

profile of v0, /device:TPU:0, one launch (start us, length us, event | category | flops | bytes accessed | tf_op | source)
XLA Modules:
  0.0 46.4 jit_solution(1926495467496724335)
XLA Ops:
  0.0 44.1 %shard_map.64 = (bf16[8,32,1024]{2,1,0:T(8,128)(2,1)}, f32[8,32,128]{2,1,0:T(8,128)}) custom-call(s32[1,8]{1,0:T(1,128)} %sizes_ref.1, bf16[8,128]{1,0:T(8,128)(2,1)} %bitcast.7, bf16[2,2048,128]{2,1,0:T(8,128)(2,1)} %bitcast.4, bf16[2,2048,128]{2,1,0:T(8,128)(2,1)} %bitcast.5, s32[8,1024]{1,0:T(8,128)} %bitcast.6), custom_call_target="tpu_custom_call" | custom-call | tf_op jit(solution)/shard_map/pallas_call | solution.py:442
  44.1 2.3 %shard_map.65 = bf16[1,3,1024,128]{3,2,1,0:T(8,128)(2,1)} custom-call(s32[1,8]{1,0:T(1,128)} %owners_ref.1, bf16[8,32,1024]{2,1,0:T(8,128)(2,1)} %get-tuple-element.7.p_ref, f32[8,32,128]{2,1,0:T(8,128)} %get-tuple-element.8.x_ref), custom_call_target="tpu_custom_call" | custom-call | tf_op jit(solution)/shard_map/pallas_call | solution.py:498
where the time goes:
time: 46.8 us; the launch traced here: 46.4 us
  Pallas kernels  46.4 us (99%)
    pallas_call x1, Pallas kernels, on_device(): pl.pallas_call(fit_kernel, out_shape=(jax.ShapeDtypeStruct((fits, rows, c...  44.1 us
    pallas_call x1, Pallas kernels, on_device(): pl.pallas_call(place_kernel, out_shape=jax.ShapeDtypeStruct((1, SLOTS, ca...  2.33 us

commit v1 on v0

--- a/solution.py
+++ b/solution.py
@@ -12,6 +12,7 @@
 FAR = -(2.0**100)
 LOG2E = 1.4426950408889634
 PAIR = 2
+BAND = 32
 
 SUBLANES = 8
 MESH = pl.DeviceIdType.MESH
@@ -84,7 +85,7 @@
 
 def fit_kernel(
     sizes_ref, q_in, k_hbm, v_hbm, idx_ref, p_ref, x_ref,
-    piece, column, table, k_ref, v_ref, s_ref, g_ref, part, part_in, chunk_mine, chunks, e_out, e_in, z_out, z_in,
+    piece, column, table, k_ref, v_ref, s_ref, g_ref, high_ref, low_ref, t_ref, part, part_in, chunk_mine, chunks, e_out, e_in, z_out, z_in,
     p_mine, p_all, x_mine, x_all,
     load, send_head, recv_head, send_seq, recv_seq, send_part, recv_part, send_chunk, recv_chunk, send_e, recv_e, send_z, recv_z,
     send_p, recv_p, send_f, recv_f, send_x, recv_x,
@@ -167,33 +168,56 @@
     def produce(fit):
         layer = fit // FITS_LAYER
         size = sizes_ref[0, fit]
-
-        def one_tile(tile, top):
-            base = pl.multiple_of(tile * LANES, LANES)
-            drawn = idx_ref[:, pl.ds(base, LANES)]
-            mine = lax.broadcasted_iota(jnp.int32, (fits, LANES), 0) == fit
-            offset = jnp.sum(jnp.where(mine, drawn, 0), axis=0, keepdims=True) - start
-            column = base + lax.broadcasted_iota(jnp.int32, (1, LANES), 1)
-            inside = (offset >= 0) & (offset < local_len) & (column < size)
-            offset = jnp.broadcast_to(jnp.where(inside, offset, -1), (rows, LANES))
-            high = offset >> 7
-            low = offset & (LANES - 1)
-            picked = jnp.full((rows, LANES), FAR, jnp.float32)
-            for block in range(local_len // LANES):
-                scored = s_ref[layer, :, block * LANES : (block + 1) * LANES]
-                found = jnp.take_along_axis(scored, low, axis=1, mode="promise_in_bounds")
-                picked = jnp.where(high == block, found, picked)
-            g_ref[:, pl.ds(base, LANES)] = picked
-            return jnp.maximum(top, jnp.max(picked, axis=1, keepdims=True))
-
-        top = lax.fori_loop(
-            0,
-            capacity // LANES,
-            one_tile,
-            jnp.full((rows, 1), FAR, jnp.float32),
-            unroll=4 if rows <= 64 else 1,
-        )
-        top = jnp.ceil(top)
+        offset = idx_ref[pl.ds(fit, 1), :] - start
+        position = lax.broadcasted_iota(jnp.int32, (1, capacity), 1)
+        inside = (offset >= 0) & (offset < local_len) & (position < size)
+        high_ref[...] = jnp.broadcast_to(
+            jnp.where(inside, offset >> 7, -1), (SUBLANES, capacity)
+        )
+        low_ref[...] = jnp.broadcast_to(offset & (LANES - 1), (SUBLANES, capacity))
+        band = min(rows, BAND)
+
+        def one_band(base_row):
+            def one_tile(tile, top):
+                base = pl.multiple_of(tile * LANES, LANES)
+                high = high_ref[:, pl.ds(base, LANES)]
+                low = low_ref[:, pl.ds(base, LANES)]
+                picked = [jnp.full((SUBLANES, LANES), FAR, jnp.float32)] * (band // SUBLANES)
+                for block in range(local_len // LANES):
+                    here = high == block
+                    for group in range(band // SUBLANES):
+                        scored = s_ref[
+                            layer,
+                            pl.ds(base_row + group * SUBLANES, SUBLANES),
+                            block * LANES : (block + 1) * LANES,
+                        ]
+                        found = jnp.take_along_axis(
+                            scored, low, axis=1, mode="promise_in_bounds"
+                        )
+                        picked[group] = jnp.where(here, found, picked[group])
+                joined = jnp.concatenate(picked, axis=0)
+                g_ref[pl.ds(base_row, band), pl.ds(base, LANES)] = joined
+                return jnp.maximum(top, joined)
+
+            top = lax.fori_loop(
+                0,
+                capacity // LANES,
+                one_tile,
+                jnp.full((band, LANES), FAR, jnp.float32),
+                unroll=True if rows == band else 1,
+            )
+            t_ref[pl.ds(base_row, band), :] = top
+
+        if rows == band:
+            one_band(0)
+        else:
+
+            def step(at, carry):
+                one_band(pl.multiple_of(at * band, band))
+                return carry
+
+            lax.fori_loop(0, rows // band, step, 0)
+        top = jnp.ceil(jnp.max(t_ref[...], axis=1, keepdims=True))
         picked = g_ref[...]
         return jnp.where(picked > 0.5 * FAR, jnp.exp2(picked - top), 0.0), top
 
@@ -455,6 +479,9 @@
             pltpu.VMEM((layers, local_len, width), jnp.bfloat16),
             pltpu.VMEM((layers, rows, local_len), jnp.float32),
             pltpu.VMEM((rows, capacity), jnp.float32),
+            pltpu.VMEM((SUBLANES, capacity), jnp.int32),
+            pltpu.VMEM((SUBLANES, capacity), jnp.int32),
+            pltpu.VMEM((rows, LANES), jnp.float32),
             pltpu.VMEM((groups, 2, chunk, width), jnp.float32),
             pltpu.VMEM((groups, 2, chunk, width), jnp.float32),
             pltpu.VMEM((chunk, width), jnp.float32),

time: 46.8 us -> 44 us (0.940)
  Pallas kernels: 46.4 us -> 43.7 us
    pallas_call x1, Pallas kernels: 44.1 us -> 41.6 us  [on_device(): pl.pallas_call(fit_kernel, out_shape=(jax.ShapeDtypeStruct((fits, rows, c...]
where the time goes in v1:
time: 44 us; the launch traced here: 43.7 us
  Pallas kernels  43.7 us (99%)
    pallas_call x1, Pallas kernels, on_device(): pl.pallas_call(fit_kernel, out_shape=(jax.ShapeDtypeStruct((fits, rows, c...  41.6 us
    pallas_call x1, Pallas kernels, on_device(): pl.pallas_call(place_kernel, out_shape=jax.ShapeDtypeStruct((1, SLOTS, ca...  2.11 us

profile of v1, /device:TPU:0, one launch (start us, length us, event | category | flops | bytes accessed | tf_op | source)
XLA Modules:
  0.0 43.7 jit_solution(9592252290015488248)
XLA Ops:
  0.0 41.6 %shard_map.64 = (bf16[8,32,1024]{2,1,0:T(8,128)(2,1)}, f32[8,32,128]{2,1,0:T(8,128)}) custom-call(s32[1,8]{1,0:T(1,128)} %sizes_ref.1, bf16[8,128]{1,0:T(8,128)(2,1)} %bitcast.7, bf16[2,2048,128]{2,1,0:T(8,128)(2,1)} %bitcast.4, bf16[2,2048,128]{2,1,0:T(8,128)(2,1)} %bitcast.5, s32[8,1024]{1,0:T(8,128)} %bitcast.6), custom_call_target="tpu_custom_call" | custom-call | tf_op jit(solution)/shard_map/pallas_call | solution.py:466
  41.6 2.1 %shard_map.65 = bf16[1,3,1024,128]{3,2,1,0:T(8,128)(2,1)} custom-call(s32[1,8]{1,0:T(1,128)} %owners_ref.1, bf16[8,32,1024]{2,1,0:T(8,128)(2,1)} %get-tuple-element.7.p_ref, f32[8,32,128]{2,1,0:T(8,128)} %get-tuple-element.8.x_ref), custom_call_target="tpu_custom_call" | custom-call | tf_op jit(solution)/shard_map/pallas_call | solution.py:525

commit v2 on v1

v2 whole, which is shorter than its diff:
```python
import jax
import jax.numpy as jnp
from jax import lax
from jax.experimental import pallas as pl
from jax.experimental.pallas import tpu as pltpu
from jax.sharding import PartitionSpec as P

FITS_LAYER = 4
SLOTS = 3
RIDGE = 0.3
LANES = 128
FAR = -(2.0**100)
LOG2E = 1.4426950408889634
PAIR = 2
BAND = 32
PANEL = 8
STEP = 0.95
HOP = 2.55
SOLVE = 3.6

SUBLANES = 8
MESH = pl.DeviceIdType.MESH
NT = (((1,), (1,)), ((), ()))
TN = (((0,), (0,)), ((), ()))


def eliminate(system, target, first, last):
    rows = system.shape[0]
    row = lax.broadcasted_iota(jnp.int32, (rows, 1), 0)
    for begin in range(first, last, PANEL):
        size = min(PANEL, last - begin)
        columns = [
            jnp.broadcast_to(system[:, k : k + 1], (rows, LANES)) for k in range(begin, begin + size)
        ]
        for at in range(size):
            k = begin + at
            column = columns[at]
            inverse = 1.0 / column[k : k + 1]
            pivot_s = system[k : k + 1] * inverse
            pivot_t = target[k : k + 1] * inverse
            column = jnp.where(row == k, column - 1.0, column)
            for later in range(at + 1, size):
                columns[later] = columns[later] - column * (columns[later][k : k + 1] * inverse)
            system = system - column * pivot_s
            target = target - column * pivot_t
    return system, target


def solve_rows(system, target):
    rows = system.shape[0]
    row = lax.broadcasted_iota(jnp.int32, (rows, 1), 0)
    lane = lax.broadcasted_iota(jnp.int32, (1, rows), 1)

    def step(k, state):
        system, target = state
        column = jnp.sum(jnp.where(lane == k, system, 0.0), axis=1, keepdims=True)
        here = row == k
        inverse = 1.0 / jnp.sum(jnp.where(here, column, 0.0), axis=0, keepdims=True)
        pivot_s = jnp.sum(jnp.where(here, system, 0.0), axis=0, keepdims=True) * inverse
        pivot_t = jnp.sum(jnp.where(here, target, 0.0), axis=0, keepdims=True) * inverse
        column = jnp.where(here, column - 1.0, column)
        return system - column * pivot_s, target - column * pivot_t

    return lax.fori_loop(0, rows, step, (system, target))[1]


def top_of(tail):
    tail = tail.astype(jnp.float32)
    return tail[:, 0:1] + tail[:, 64:65]


def tail_of(top):
    lane = lax.broadcasted_iota(jnp.int32, (top.shape[0], LANES), 1)
    high = top.astype(jnp.bfloat16)
    low = (top - high.astype(jnp.float32)).astype(jnp.bfloat16)
    return jnp.where(lane < 64, high.astype(jnp.float32), low.astype(jnp.float32)).astype(
        jnp.bfloat16
    )


def others():
    heads, groups = lax.axis_size("head"), lax.axis_size("seq")
    my_head, me = lax.axis_index("head"), lax.axis_index("seq")
    for shift in range(heads):
        for step in range(groups):
            if shift or step:
                yield (
                    shift * groups + step,
                    lax.rem(my_head + shift, heads),
                    lax.rem(me + step, groups),
                )


def greet():
    barrier = pltpu.get_barrier_semaphore()
    for _, head, seq in others():
        pl.semaphore_signal(
            barrier, inc=1, device_id={"head": head, "seq": seq}, device_id_type=MESH
        )


def admit():
    pl.semaphore_wait(
        pltpu.get_barrier_semaphore(), lax.axis_size("head") * lax.axis_size("seq") - 1
    )


def send(source, target, send_sem, recv_sem, peer, head=None):
    return pltpu.make_async_remote_copy(
        src_ref=source,
        dst_ref=target,
        send_sem=send_sem,
        recv_sem=recv_sem,
        device_id={"seq": peer} if head is None else {"head": head, "seq": peer},
        device_id_type=MESH,
    )


def fit_kernel(
    sizes_hbm, owners_hbm, q_hbm, k_hbm, v_hbm, idx_hbm, p_ref, x_ref,
    sizes_ref, owners_ref, q_in, idx_ref,
    piece, table, k_ref, v_ref, s_ref, g_ref, high_ref, low_ref, t_ref,
    part, part_in, chunk_mine, chunks, gram_out, gram_in,
    e_out, e_in, pair, both, z_out, z_in, p_all, x_mine, x_all,
    load, send_q, recv_q, send_part, recv_part, send_chunk, recv_chunk, send_gram, recv_gram,
    send_e, recv_e, send_z, recv_z, send_p, recv_p, send_x, recv_x,
):
    layers, local_len, width = k_ref.shape
    fits, capacity = idx_ref.shape
    heads, my_head = lax.axis_size("head"), lax.axis_index("head")
    groups, me = lax.axis_size("seq"), lax.axis_index("seq")
    rows = groups * heads
    outer, inner = me // PAIR, lax.rem(me, PAIR)
    outers, half = groups // PAIR, fits // PAIR
    partner = outer * PAIR + 1 - inner
    fit_mine = jnp.minimum(me, fits - 1)
    chunk = layers * rows // groups
    start = me * local_len
    lane = lax.broadcasted_iota(jnp.int32, (rows, LANES), 1)
    near = (outer >= outers // 2).astype(jnp.int32)
    far = 1 - near
    inside_line = (outer > 0) & (outer < outers - 1)
    wide = gram_in.shape[2]
    middle = (rows + wide) // 2

    loads = [
        pltpu.make_async_copy(k_hbm, k_ref, load.at[0]),
        pltpu.make_async_copy(v_hbm, v_ref, load.at[1]),
        pltpu.make_async_copy(idx_hbm, idx_ref, load.at[2]),
        pltpu.make_async_copy(q_hbm, q_in, load.at[3]),
        pltpu.make_async_copy(sizes_hbm, sizes_ref, load.at[4]),
        pltpu.make_async_copy(owners_hbm, owners_ref, load.at[5]),
    ]
    loads[3].start()
    greet()
    for at in (4, 5, 2, 0, 1):
        loads[at].start()
    loads[3].wait()
    drawn_rows = q_in[...].astype(jnp.float32)
    for head in range(heads):
        for layer in range(layers):
            at = layer * heads + head
            piece[head, layer : layer + 1, :] = drawn_rows[at : at + 1]
    admit()
    my_row = me * heads + my_head
    asked = []
    for at, head, seq in others():
        asked.append(
            send(piece.at[head], table.at[my_row], send_q.at[at], recv_q.at[at], seq, head)
        )
        asked[-1].start()
    table[my_row] = piece[my_head]
    for copy in asked:
        copy.wait_recv()
    for at in (0, 2, 4, 5):
        loads[at].wait()
    for layer in range(layers):
        query_rows = table[:, layer, :].astype(jnp.bfloat16)
        s_ref[layer] = lax.dot_general(
            query_rows, k_ref[layer], NT, preferred_element_type=jnp.float32
        ) * (width ** (-0.5) * LOG2E)

    parts = [
        send(
            part.at[lax.rem(me + step, groups)], part_in.at[step],
            send_part.at[step], recv_part.at[step], lax.rem(me + step, groups),
        )
        for step in range(1, groups)
    ]

    def attend():
        loads[1].wait()
        for layer in range(layers):
            scores = s_ref[layer]
            peak = jnp.max(scores, axis=1, keepdims=True)
            weights = jnp.exp2(scores - peak)
            total = jnp.sum(weights, axis=1, keepdims=True)
            numer = jnp.dot(
                weights.astype(jnp.bfloat16), v_ref[layer], preferred_element_type=jnp.float32
            )
            side = jnp.where(lane < 64, total, peak)
            for at in range(rows // chunk):
                slot = layer * (rows // chunk) + at
                part[slot, 0] = numer[at * chunk : (at + 1) * chunk]
                part[slot, 1] = side[at * chunk : (at + 1) * chunk]
        for copy in parts:
            copy.start()
        part_in[0] = part[me]

    def produce(fit):
        layer = fit // FITS_LAYER
        size = sizes_ref[0, fit]
        offset = idx_ref[pl.ds(fit, 1), :] - start
        position = lax.broadcasted_iota(jnp.int32, (1, capacity), 1)
        inside = (offset >= 0) & (offset < local_len) & (position < size)
        high_ref[...] = jnp.broadcast_to(
            jnp.where(inside, offset >> 7, -1), (SUBLANES, capacity)
        )
        low_ref[...] = jnp.broadcast_to(offset & (LANES - 1), (SUBLANES, capacity))
        band = min(rows, BAND)

        def one_band(base_row):
            def one_tile(tile, top):
                base = pl.multiple_of(tile * LANES, LANES)
                high = high_ref[:, pl.ds(base, LANES)]
                low = low_ref[:, pl.ds(base, LANES)]
                picked = [jnp.full((SUBLANES, LANES), FAR, jnp.float32)] * (band // SUBLANES)
                for block in range(local_len // LANES):
                    here = high == block
                    for group in range(band // SUBLANES):
                        scored = s_ref[
                            layer,
                            pl.ds(base_row + group * SUBLANES, SUBLANES),
                            block * LANES : (block + 1) * LANES,
                        ]
                        found = jnp.take_along_axis(
                            scored, low, axis=1, mode="promise_in_bounds"
                        )
                        picked[group] = jnp.where(here, found, picked[group])
                joined = jnp.concatenate(picked, axis=0)
                g_ref[pl.ds(base_row, band), pl.ds(base, LANES)] = joined
                return jnp.maximum(top, joined)

            top = lax.fori_loop(
                0,
                capacity // LANES,
                one_tile,
                jnp.full((band, LANES), FAR, jnp.float32),
                unroll=True if rows == band else 1,
            )
            t_ref[pl.ds(base_row, band), :] = top

        if rows == band:
            one_band(0)
        else:

            def step(at, carry):
                one_band(pl.multiple_of(at * band, band))
                return carry

            lax.fori_loop(0, rows // band, step, 0)
        top = jnp.ceil(jnp.max(t_ref[...], axis=1, keepdims=True))
        picked = g_ref[...]
        return jnp.where(picked > 0.5 * FAR, jnp.exp2(picked - top), 0.0), top

    gram_lane = lax.broadcasted_iota(jnp.int32, (rows, wide), 1)

    def gram_copy(at, fit):
        return send(gram_out.at[at], gram_in.at[me], send_gram.at[at], recv_gram.at[me], fit)

    def fill_gram(at, expo, top):
        total = jnp.sum(expo.astype(jnp.float32), axis=1, keepdims=True)
        gram_out[at] = jnp.where(gram_lane >= middle, top, total)
        gram_out[at, :, :rows] = lax.dot_general(
            expo, expo, NT, preferred_element_type=jnp.float32
        )

    cut = capacity // 2
    spans = (slice(cut, capacity + LANES), slice(0, cut))
    plain = (slice(cut, capacity), slice(0, cut))
    gives = [j * PAIR + 1 - inner for j in range(half)]
    keeps = [j * PAIR + inner for j in range(half)]

    def cross(j, q):
        return send(
            e_out.at[j, :, spans[q]], e_in.at[j, :, spans[q]],
            send_e.at[j, q], recv_e.at[j, q], partner,
        )

    def stream(way, j, q):
        return send(
            z_out.at[way, j, :, spans[q]], z_in.at[way, j, :, spans[q]],
            send_z.at[way, j, q], recv_z.at[way, j, q],
            lax.rem(me + PAIR * (1 - 2 * way) + groups, groups),
        )

    def onward(j, q):
        return send(
            p_all.at[keeps[j], :, plain[q]], p_all.at[keeps[j], :, plain[q]],
            send_p.at[j, q], recv_p.at[j, q], partner,
        )

    def blend(one, other, at):
        first, second = top_of(one[:, capacity:]), top_of(other[:, capacity:])
        top = jnp.maximum(first, second)
        return (
            one[:, at] * jnp.exp2(first - top).astype(jnp.bfloat16)
            + other[:, at] * jnp.exp2(second - top).astype(jnp.bfloat16)
        ), top

    def put(ref, q, mixed):
        ref[:, plain[q]] = mixed[0]
        if q == 0:
            ref[:, capacity:] = tail_of(mixed[1])

    def give(j):
        expo, top = produce(gives[j])
        expo = expo.astype(jnp.bfloat16)
        e_out[j, :, :capacity] = expo
        e_out[j, :, capacity:] = tail_of(top)
        for q in range(2):
            cross(j, q).start()
        fill_gram(j, expo, top)
        gram_copy(j, gives[j]).start()

    def keep(j):
        expo, top = produce(keeps[j])
        expo = expo.astype(jnp.bfloat16)
        pair[j, :, :capacity] = expo
        pair[j, :, capacity:] = tail_of(top)
        fill_gram(half + j, expo, top)
        pl.when(keeps[j] != me)(gram_copy(half + j, keeps[j]).start)

    def join(j, q):
        cross(j, q).wait_recv()
        mixed = blend(pair.at[j], e_in.at[j], plain[q])
        put(both.at[j], q, mixed)

        @pl.when(~inside_line)
        def _():
            put(z_out.at[near, j], q, mixed)
            stream(near, j, q).start()

    def pass_near(j, q):

        @pl.when(inside_line)
        def _():
            stream(near, j, q).wait_recv()
            put(z_out.at[near, j], q, blend(both.at[j], z_in.at[near, j], plain[q]))
            stream(near, j, q).start()

    def pass_far(j, q):
        stream(far, j, q).wait_recv()

        @pl.when(inside_line)
        def _():
            put(z_out.at[far, j], q, blend(both.at[j], z_in.at[far, j], plain[q]))
            stream(far, j, q).start()

        p_all[keeps[j], :, plain[q]] = blend(z_out.at[near, j], z_in.at[far, j], plain[q])[0]
        onward(j, q).start()

    def merge_targets():
        for copy in parts:
            copy.wait_recv()
        peak = part_in[0, 1][:, 64:65]
        for step in range(1, groups):
            peak = jnp.maximum(peak, part_in[step, 1][:, 64:65])
        numer, total = 0.0, 0.0
        for step in range(groups):
            factor = jnp.exp2(part_in[step, 1][:, 64:65] - peak)
            numer = numer + part_in[step, 0] * factor
            total = total + part_in[step, 1][:, 0:1] * factor
        target = numer / total
        chunk_mine[...] = target
        chunks[me] = target
        for copy in spread:
            copy.start()

    spread = [
        send(
            chunk_mine, chunks.at[me], send_chunk.at[step], recv_chunk.at[step],
            lax.rem(me + step, groups),
        )
        for step in range(1, groups)
    ]
    results = [
        send(
            x_mine, x_all.at[fit_mine], send_x.at[step], recv_x.at[step],
            lax.rem(me + step, groups),
        )
        for step in range(1, groups)
    ]

    def only(condition, act):
        if groups == fits:
            act()
        else:
            pl.when(condition)(act)

    def gather_system():
        for copy in spread:
            copy.wait_recv()

        def wait_grams():
            for step in range(1, groups):
                source = lax.rem(me + step, groups)
                send(
                    gram_out.at[0], gram_in.at[source], send_gram.at[0], recv_gram.at[source], source
                ).wait_recv()

        only(me < fits, wait_grams)

    state = {}

    def assemble():
        diagonal = lax.broadcasted_iota(jnp.int32, (rows, wide), 0) == lax.broadcasted_iota(
            jnp.int32, (rows, wide), 1
        )

        def across_lanes(column):
            return jnp.sum(jnp.where(diagonal, column, 0.0), axis=0, keepdims=True)

        gram_in[me] = gram_out[half + jnp.minimum(outer, half - 1)]
        tops = [gram_in[source, :, middle : middle + 1] for source in range(groups)]
        top = tops[0]
        for other in tops[1:]:
            top = jnp.maximum(top, other)
        gram, total = 0.0, 0.0
        for source in range(groups):
            factor = jnp.exp2(tops[source] - top)
            total = total + factor * gram_in[source, :, rows : rows + 1]
            gram = gram + gram_in[source] * factor * across_lanes(factor)
        scale = 1.0 / total
        gram = jnp.where(gram_lane < rows, gram * scale * across_lanes(scale), 0.0)
        trace = jnp.sum(jnp.where(diagonal, gram, 0.0))
        ridge = RIDGE * trace / sizes_ref[0, fit_mine].astype(jnp.float32)
        span = rows // chunk
        base = (fit_mine // FITS_LAYER) * span
        target = jnp.concatenate([chunks[base + at] for at in range(span)], axis=0)
        state["target"] = target.astype(jnp.bfloat16).astype(jnp.float32)
        state["system"] = jnp.where(diagonal, gram + ridge, gram)
        state["scale"] = scale

    def conclude(solved):
        solved = solved * state["scale"]
        x_mine[...] = solved
        x_all[fit_mine] = solved
        for copy in results:
            copy.start()

    small = rows <= 64 and groups == fits

    def solve_first():
        gather_system()
        if small:
            assemble()
            state["system"], state["target"] = eliminate(
                state["system"], state["target"], 0, rows // 2
            )

    def solve_last():
        if small:
            conclude(eliminate(state["system"], state["target"], rows // 2, rows)[1])
        else:

            def whole():
                assemble()
                conclude(solve_rows(state["system"][:, :rows], state["target"]))

            only(me < fits, whole)

    agenda = [(1.54, attend, ()), (4.65, merge_targets, ())]
    agenda += [(10.23, solve_first, ()), (10.7, solve_last, ())]
    for j in range(half):
        agenda += [(1.62 * j, give, (j,)), (3.0 + 1.22 * j, keep, (j,))]
        for q in range(2):
            at = 3.42 + 1.17 * j + 0.4 * q
            agenda.append((at, join, (j, q)))
            agenda.append((at + 2.16, pass_near, (j, q)))
            agenda.append((at + 4.75, pass_far, (j, q)))
    for _, act, at in sorted(agenda, key=lambda entry: entry[0]):
        act(*at)
    halves = [(j, q) for j in range(half) for q in range(2)]
    for copy in asked + parts + spread:
        copy.wait_send()
    for j, q in halves:
        cross(j, q).wait_send()
        onward(j, q).wait_send()
    for at, fit in enumerate(gives + keeps):
        if at < half:
            gram_copy(at, fit).wait_send()
        else:
            pl.when(fit != me)(gram_copy(at, fit).wait_send)
    for j, q in halves:
        stream(near, j, q).wait_send()
        pl.when(inside_line)(stream(far, j, q).wait_send)
    for j, q in halves:
        onward(j, q).wait_recv()
    for step in range(1, groups):
        source = lax.rem(me + groups - step, groups)
        only(source < fits, results[step - 1].wait_recv)
        only(me < fits, results[step - 1].wait_send)
    count = jnp.int32(0)
    chosen = [jnp.int32(0)] * SLOTS
    for fit in range(fits):
        mine = owners_ref[0, fit] == me
        for slot in range(SLOTS):
            chosen[slot] = jnp.where(mine & (count == slot), fit, chosen[slot])
        count = count + mine.astype(jnp.int32)
    for slot in range(SLOTS):
        p_ref[slot] = p_all[chosen[slot]]
        x_ref[slot] = jnp.where(count > slot, x_all[chosen[slot]], 0.0)


def place_kernel(p_ref, x_ref, out_hbm, out_ref, store):
    stores = []
    for slot in range(SLOTS):
        probs = p_ref[slot]
        rows = x_ref[slot]
        high = rows.astype(jnp.bfloat16)
        low = (rows - high.astype(jnp.float32)).astype(jnp.bfloat16)
        out_ref[slot] = lax.dot_general(
            jnp.concatenate([probs, probs], axis=0),
            jnp.concatenate([high, low], axis=0),
            TN,
            preferred_element_type=jnp.float32,
        ).astype(jnp.bfloat16)
        stores.append(pltpu.make_async_copy(out_ref.at[slot], out_hbm.at[0, slot], store.at[slot]))
        stores[-1].start()
    for copy in stores:
        copy.wait()


VMEM = pl.BlockSpec(memory_space=pltpu.VMEM)
ANY = pl.BlockSpec(memory_space=pl.ANY)


def on_device(queries, keys, values, indices, sizes, owners):
    layers, heads, count, width = queries.shape
    groups = lax.axis_size("seq")
    rows = groups * heads * count
    local_len = keys.shape[2]
    fits, capacity = indices.shape[1:]
    dma = pltpu.SemaphoreType.DMA
    params = dict(vmem_limit_bytes=(24 + rows // 8) * 1024 * 1024)
    half = fits // PAIR
    chunk = layers * rows // groups
    wide = (rows // LANES + 1) * LANES
    packed = (rows, capacity + LANES)
    probs, solved = pl.pallas_call(
        fit_kernel,
        out_shape=(
            jax.ShapeDtypeStruct((SLOTS, rows, capacity), jnp.bfloat16),
            jax.ShapeDtypeStruct((SLOTS, rows, width), jnp.float32),
        ),
        in_specs=[ANY] * 6,
        out_specs=(VMEM, VMEM),
        scratch_shapes=[
            pltpu.SMEM((1, fits), jnp.int32),
            pltpu.SMEM((1, fits), jnp.int32),
            pltpu.VMEM((layers * heads, width), queries.dtype),
            pltpu.VMEM((fits, capacity), jnp.int32),
            pltpu.VMEM((heads, layers, width), jnp.float32),
            pltpu.VMEM((rows, layers, width), jnp.float32),
            pltpu.VMEM((layers, local_len, width), jnp.bfloat16),
            pltpu.VMEM((layers, local_len, width), jnp.bfloat16),
            pltpu.VMEM((layers, rows, local_len), jnp.float32),
            pltpu.VMEM((rows, capacity), jnp.float32),
            pltpu.VMEM((SUBLANES, capacity), jnp.int32),
            pltpu.VMEM((SUBLANES, capacity), jnp.int32),
            pltpu.VMEM((rows, LANES), jnp.float32),
            pltpu.VMEM((groups, 2, chunk, width), jnp.float32),
            pltpu.VMEM((groups, 2, chunk, width), jnp.float32),
            pltpu.VMEM((chunk, width), jnp.float32),
            pltpu.VMEM((groups, chunk, width), jnp.float32),
            pltpu.VMEM((fits, rows, wide), jnp.float32),
            pltpu.VMEM((groups, rows, wide), jnp.float32),
            pltpu.VMEM((half,) + packed, jnp.bfloat16),
            pltpu.VMEM((half,) + packed, jnp.bfloat16),
            pltpu.VMEM((half,) + packed, jnp.bfloat16),
            pltpu.VMEM((half,) + packed, jnp.bfloat16),
            pltpu.VMEM((2, half) + packed, jnp.bfloat16),
            pltpu.VMEM((2, half) + packed, jnp.bfloat16),
            pltpu.VMEM((fits, rows, capacity), jnp.bfloat16),
            pltpu.VMEM((rows, width), jnp.float32),
            pltpu.VMEM((fits, rows, width), jnp.float32),
            dma((6,)),
            dma((heads * groups,)),
            dma((heads * groups,)),
            dma((groups,)),
            dma((groups,)),
            dma((groups,)),
            dma((groups,)),
            dma((fits,)),
            dma((groups,)),
            dma((half, 2)),
            dma((half, 2)),
            dma((2, half, 2)),
            dma((2, half, 2)),
            dma((half, 2)),
            dma((half, 2)),
            dma((groups,)),
            dma((groups,)),
        ],
        compiler_params=pltpu.CompilerParams(collective_id=2, has_side_effects=True, **params),
    )(
        *(
            pltpu.with_memory_space_constraint(array, pltpu.HBM)
            for array in (
                sizes,
                owners,
                queries.reshape(layers * heads, width),
                keys[:, 0],
                values[:, 0],
                indices[0],
            )
        )
    )
    return pl.pallas_call(
        place_kernel,
        out_shape=jax.ShapeDtypeStruct((1, SLOTS, capacity, width), jnp.bfloat16),
        in_specs=[VMEM, VMEM],
        out_specs=ANY,
        scratch_shapes=[pltpu.VMEM((SLOTS, capacity, width), jnp.bfloat16), dma((SLOTS,))],
        compiler_params=pltpu.CompilerParams(**params),
    )(probs, solved)


def solution(mesh):
    in_specs = (
        P(None, None, ("head", "seq"), None),
        P(None, "head", "seq", None),
        P(None, "head", "seq", None),
        P("head", None, None),
        P("head", None),
        P("head", None),
    )
    out_specs = P("head", "seq", None, None)
    return jax.shard_map(
        on_device, mesh=mesh, in_specs=in_specs, out_specs=out_specs, check_vma=False
    )
```

time: 44 us -> 40.2 us (0.914)
  Pallas kernels: 43.7 us -> 40 us
    pallas_call x1, Pallas kernels: 41.6 us -> 38.8 us  [on_device(): pl.pallas_call(fit_kernel, out_shape=(jax.ShapeDtypeStruct((SLOTS, rows,...]
    pallas_call x1, Pallas kernels: 2.11 us -> 1.22 us  [on_device(): pl.pallas_call(place_kernel, out_shape=jax.ShapeDtypeStruct((1, SLOTS, ca...]
where the time goes in v2:
time: 40.2 us; the launch traced here: 40 us
  Pallas kernels  40 us (100%)
    pallas_call x1, Pallas kernels, on_device(): pl.pallas_call(fit_kernel, out_shape=(jax.ShapeDtypeStruct((SLOTS, rows,...  38.8 us
    pallas_call x1, Pallas kernels, on_device(): pl.pallas_call(place_kernel, out_shape=jax.ShapeDtypeStruct((1, SLOTS, ca...  1.22 us

profile of v2, /device:TPU:0, one launch (start us, length us, event | category | flops | bytes accessed | tf_op | source)
XLA Modules:
  0.0 40.0 jit_solution(122432722764133789)
XLA Ops:
  0.0 38.8 %shard_map.64 = (bf16[3,32,1024]{2,1,0:T(8,128)(2,1)S(1)}, f32[3,32,128]{2,1,0:T(8,128)S(1)}) custom-call(s32[1,8]{1,0:T(1,128)} %sizes_hbm.1, s32[1,8]{1,0:T(1,128)} %owners_hbm.1, bf16[8,128]{1,0:T(8,128)(2,1)} %bitcast.7, bf16[2,2048,128]{2,1,0:T(8,128)(2,1)} %bitcast.4, bf16[2,2048,128]{2,1,0:T(8,128)(2,1)} %bitcast.5, s32[8,1024]{1,0:T(8,128)} %bitcast.6), custom_call_target="tpu_custom_call" | custom-call | tf_op jit(solution)/shard_map/pallas_call | solution.py:551
  38.8 1.2 %shard_map.65 = bf16[1,3,1024,128]{3,2,1,0:T(8,128)(2,1)} custom-call(bf16[3,32,1024]{2,1,0:T(8,128)(2,1)S(1)} %get-tuple-element.7.p_ref, f32[3,32,128]{2,1,0:T(8,128)S(1)} %get-tuple-element.8.x_ref), custom_call_target="tpu_custom_call" | custom-call | tf_op jit(solution)/shard_map/pallas_call | solution.py:620

commit v3 on v2

--- a/solution.py
+++ b/solution.py
@@ -13,6 +13,7 @@
 LOG2E = 1.4426950408889634
 PAIR = 2
 BAND = 32
+COARSE = 8.0
 PANEL = 8
 STEP = 0.95
 HOP = 2.55
@@ -62,20 +63,6 @@
         return system - column * pivot_s, target - column * pivot_t
 
     return lax.fori_loop(0, rows, step, (system, target))[1]
-
-
-def top_of(tail):
-    tail = tail.astype(jnp.float32)
-    return tail[:, 0:1] + tail[:, 64:65]
-
-
-def tail_of(top):
-    lane = lax.broadcasted_iota(jnp.int32, (top.shape[0], LANES), 1)
-    high = top.astype(jnp.bfloat16)
-    low = (top - high.astype(jnp.float32)).astype(jnp.bfloat16)
-    return jnp.where(lane < 64, high.astype(jnp.float32), low.astype(jnp.float32)).astype(
-        jnp.bfloat16
-    )
 
 
 def others():
@@ -166,12 +153,12 @@
     asked = []
     for at, head, seq in others():
         asked.append(
-            send(piece.at[head], table.at[my_row], send_q.at[at], recv_q.at[at], seq, head)
+            send(piece.at[head], table.at[my_row], send_q, recv_q, seq, head)
         )
         asked[-1].start()
     table[my_row] = piece[my_head]
-    for copy in asked:
-        copy.wait_recv()
+    every = table.at[pl.ds(0, heads * groups - 1)]
+    send(every, every, send_q, recv_q, partner).wait_recv()
     for at in (0, 2, 4, 5):
         loads[at].wait()
     for layer in range(layers):
@@ -183,7 +170,7 @@
     parts = [
         send(
             part.at[lax.rem(me + step, groups)], part_in.at[step],
-            send_part.at[step], recv_part.at[step], lax.rem(me + step, groups),
+            send_part, recv_part, lax.rem(me + step, groups),
         )
         for step in range(1, groups)
     ]
@@ -259,14 +246,14 @@
                 return carry
 
             lax.fori_loop(0, rows // band, step, 0)
-        top = jnp.ceil(jnp.max(t_ref[...], axis=1, keepdims=True))
+        top = COARSE * jnp.ceil(jnp.max(t_ref[...], axis=1, keepdims=True) * (1.0 / COARSE))
         picked = g_ref[...]
         return jnp.where(picked > 0.5 * FAR, jnp.exp2(picked - top), 0.0), top
 
     gram_lane = lax.broadcasted_iota(jnp.int32, (rows, wide), 1)
 
     def gram_copy(at, fit):
-        return send(gram_out.at[at], gram_in.at[me], send_gram.at[at], recv_gram.at[me], fit)
+        return send(gram_out.at[at], gram_in.at[me], send_gram, recv_gram, fit)
 
     def fill_gram(at, expo, top):
         total = jnp.sum(expo.astype(jnp.float32), axis=1, keepdims=True)
@@ -284,34 +271,50 @@
     def cross(j, q):
         return send(
             e_out.at[j, :, spans[q]], e_in.at[j, :, spans[q]],
-            send_e.at[j, q], recv_e.at[j, q], partner,
+            send_e, recv_e.at[j, q], partner,
         )
 
     def stream(way, j, q):
         return send(
             z_out.at[way, j, :, spans[q]], z_in.at[way, j, :, spans[q]],
-            send_z.at[way, j, q], recv_z.at[way, j, q],
+            send_z.at[way], recv_z.at[way, j, q],
             lax.rem(me + PAIR * (1 - 2 * way) + groups, groups),
         )
 
     def onward(j, q):
         return send(
             p_all.at[keeps[j], :, plain[q]], p_all.at[keeps[j], :, plain[q]],
-            send_p.at[j, q], recv_p.at[j, q], partner,
+            send_p, recv_p, partner,
+        )
+
+    def sent(ref, sem):
+        send(ref, ref, sem, sem, partner).wait_send()
+
+    def came(ref, sem):
+        send(ref, ref, sem, sem, partner).wait_recv()
+
+    def scales(one, other):
+        first = one[:, capacity:].astype(jnp.float32)
+        second = other[:, capacity:].astype(jnp.float32)
+        top = jnp.maximum(first, second)
+        wide_by = cut // LANES
+        return (
+            top.astype(jnp.bfloat16),
+            jnp.concatenate([jnp.exp2(first - top).astype(jnp.bfloat16)] * wide_by, axis=1),
+            jnp.concatenate([jnp.exp2(second - top).astype(jnp.bfloat16)] * wide_by, axis=1),
         )
 
     def blend(one, other, at):
-        first, second = top_of(one[:, capacity:]), top_of(other[:, capacity:])
-        top = jnp.maximum(first, second)
-        return (
-            one[:, at] * jnp.exp2(first - top).astype(jnp.bfloat16)
-            + other[:, at] * jnp.exp2(second - top).astype(jnp.bfloat16)
-        ), top
+        top, first, second = scales(one, other)
+        return one[:, at] * first + other[:, at] * second, top
 
     def put(ref, q, mixed):
         ref[:, plain[q]] = mixed[0]
         if q == 0:
-            ref[:, capacity:] = tail_of(mixed[1])
+            ref[:, capacity:] = mixed[1]
+
+    def tail_of(top):
+        return jnp.broadcast_to(top, (rows, LANES)).astype(jnp.bfloat16)
 
     def give(j):
         expo, top = produce(gives[j])
@@ -361,8 +364,7 @@
         onward(j, q).start()
 
     def merge_targets():
-        for copy in parts:
-            copy.wait_recv()
+        came(part_in.at[pl.ds(1, groups - 1)], recv_part)
         peak = part_in[0, 1][:, 64:65]
         for step in range(1, groups):
             peak = jnp.maximum(peak, part_in[step, 1][:, 64:65])
@@ -379,14 +381,14 @@
 
     spread = [
         send(
-            chunk_mine, chunks.at[me], send_chunk.at[step], recv_chunk.at[step],
+            chunk_mine, chunks.at[me], send_chunk, recv_chunk,
             lax.rem(me + step, groups),
         )
         for step in range(1, groups)
     ]
     results = [
         send(
-            x_mine, x_all.at[fit_mine], send_x.at[step], recv_x.at[step],
+            x_mine, x_all.at[fit_mine], send_x, recv_x,
             lax.rem(me + step, groups),
         )
         for step in range(1, groups)
@@ -399,15 +401,10 @@
             pl.when(condition)(act)
 
     def gather_system():
-        for copy in spread:
-            copy.wait_recv()
+        came(chunks.at[pl.ds(0, groups - 1)], recv_chunk)
 
         def wait_grams():
-            for step in range(1, groups):
-                source = lax.rem(me + step, groups)
-                send(
-                    gram_out.at[0], gram_in.at[source], send_gram.at[0], recv_gram.at[source], source
-                ).wait_recv()
+            came(gram_in.at[pl.ds(0, groups - 1)], recv_gram)
 
         only(me < fits, wait_grams)
 
@@ -481,26 +478,26 @@
             agenda.append((at + 4.75, pass_far, (j, q)))
     for _, act, at in sorted(agenda, key=lambda entry: entry[0]):
         act(*at)
-    halves = [(j, q) for j in range(half) for q in range(2)]
-    for copy in asked + parts + spread:
-        copy.wait_send()
-    for j, q in halves:
-        cross(j, q).wait_send()
-        onward(j, q).wait_send()
-    for at, fit in enumerate(gives + keeps):
-        if at < half:
-            gram_copy(at, fit).wait_send()
-        else:
-            pl.when(fit != me)(gram_copy(at, fit).wait_send)
-    for j, q in halves:
-        stream(near, j, q).wait_send()
-        pl.when(inside_line)(stream(far, j, q).wait_send)
-    for j, q in halves:
-        onward(j, q).wait_recv()
-    for step in range(1, groups):
-        source = lax.rem(me + groups - step, groups)
-        only(source < fits, results[step - 1].wait_recv)
-        only(me < fits, results[step - 1].wait_send)
+    sent(table.at[pl.ds(0, heads * groups - 1)], send_q)
+    sent(part.at[pl.ds(0, groups - 1)], send_part)
+    sent(chunks.at[pl.ds(0, groups - 1)], send_chunk)
+    sent(e_out, send_e)
+    if groups == fits:
+        sent(gram_out.at[pl.ds(0, fits - 1)], send_gram)
+    else:
+        pl.when(me < fits)(lambda: sent(gram_out.at[pl.ds(0, fits - 1)], send_gram))
+        pl.when(me >= fits)(lambda: sent(gram_out, send_gram))
+    sent(z_out.at[near], send_z.at[near])
+    pl.when(inside_line)(lambda: sent(z_out.at[far], send_z.at[far]))
+    sent(p_all.at[pl.ds(0, half)], send_p)
+    if groups == fits:
+        came(x_all.at[pl.ds(0, fits - 1)], recv_x)
+        sent(gram_in.at[pl.ds(0, groups - 1), :, :width], send_x)
+    else:
+        pl.when(me < fits)(lambda: came(x_all.at[pl.ds(0, fits - 1)], recv_x))
+        pl.when(me < fits)(lambda: sent(gram_in.at[pl.ds(0, groups - 1), :, :width], send_x))
+        pl.when(me >= fits)(lambda: came(x_all, recv_x))
+    came(p_all.at[pl.ds(0, half)], recv_p)
     count = jnp.int32(0)
     chosen = [jnp.int32(0)] * SLOTS
     for fit in range(fits):
@@ -586,22 +583,22 @@
             pltpu.VMEM((rows, width), jnp.float32),
             pltpu.VMEM((fits, rows, width), jnp.float32),
             dma((6,)),
-            dma((heads * groups,)),
-            dma((heads * groups,)),
-            dma((groups,)),
-            dma((groups,)),
-            dma((groups,)),
-            dma((groups,)),
-            dma((fits,)),
-            dma((groups,)),
+            dma,
+            dma,
+            dma,
+            dma,
+            dma,
+            dma,
+            dma,
+            dma,
+            dma,
             dma((half, 2)),
-            dma((half, 2)),
+            dma((2,)),
             dma((2, half, 2)),
-            dma((2, half, 2)),
-            dma((half, 2)),
-            dma((half, 2)),
-            dma((groups,)),
-            dma((groups,)),
+            dma,
+            dma,
+            dma,
+            dma,
         ],
         compiler_params=pltpu.CompilerParams(collective_id=2, has_side_effects=True, **params),
     )(

time: 40.2 us -> 38.2 us (0.950)
  Pallas kernels: 40 us -> 38 us
    pallas_call x1, Pallas kernels: 38.8 us -> 36.8 us  [on_device(): pl.pallas_call(fit_kernel, out_shape=(jax.ShapeDtypeStruct((SLOTS, rows,...]
where the time goes in v3:
time: 38.2 us; the launch traced here: 38.1 us
  Pallas kernels  38 us (99%)
    pallas_call x1, Pallas kernels, on_device(): pl.pallas_call(fit_kernel, out_shape=(jax.ShapeDtypeStruct((SLOTS, rows,...  36.8 us
    pallas_call x1, Pallas kernels, on_device(): pl.pallas_call(place_kernel, out_shape=jax.ShapeDtypeStruct((1, SLOTS, ca...  1.22 us

profile of v3, /device:TPU:0, one launch (start us, length us, event | category | flops | bytes accessed | tf_op | source)
XLA Modules:
  0.0 38.1 jit_solution(17458862368688726121)
XLA Ops:
  0.0 36.8 %shard_map.64 = (bf16[3,32,1024]{2,1,0:T(8,128)(2,1)S(1)}, f32[3,32,128]{2,1,0:T(8,128)S(1)}) custom-call(s32[1,8]{1,0:T(1,128)} %sizes_hbm.1, s32[1,8]{1,0:T(1,128)} %owners_hbm.1, bf16[8,128]{1,0:T(8,128)(2,1)} %bitcast.7, bf16[2,2048,128]{2,1,0:T(8,128)(2,1)} %bitcast.4, bf16[2,2048,128]{2,1,0:T(8,128)(2,1)} %bitcast.5, s32[8,1024]{1,0:T(8,128)} %bitcast.6), custom_call_target="tpu_custom_call" | custom-call | tf_op jit(solution)/shard_map/pallas_call | solution.py:548
  36.8 1.2 %shard_map.65 = bf16[1,3,1024,128]{3,2,1,0:T(8,128)(2,1)} custom-call(bf16[3,32,1024]{2,1,0:T(8,128)(2,1)S(1)} %get-tuple-element.7.p_ref, f32[3,32,128]{2,1,0:T(8,128)S(1)} %get-tuple-element.8.x_ref), custom_call_target="tpu_custom_call" | custom-call | tf_op jit(solution)/shard_map/pallas_call | solution.py:617

commit v4 on v3

--- a/solution.py
+++ b/solution.py
@@ -252,15 +252,18 @@
 
     gram_lane = lax.broadcasted_iota(jnp.int32, (rows, wide), 1)
 
-    def gram_copy(at, fit):
-        return send(gram_out.at[at], gram_in.at[me], send_gram, recv_gram, fit)
-
-    def fill_gram(at, expo, top):
+    def gram_copy(j):
+        return send(gram_out.at[j], gram_in.at[outer], send_gram, recv_gram, keeps[j])
+
+    def fill_gram(j):
+        expo = both[j, :, :capacity]
+        top = both[j, :, capacity:].astype(jnp.float32)[:, :1]
         total = jnp.sum(expo.astype(jnp.float32), axis=1, keepdims=True)
-        gram_out[at] = jnp.where(gram_lane >= middle, top, total)
-        gram_out[at, :, :rows] = lax.dot_general(
+        gram_out[j] = jnp.where(gram_lane >= middle, top, total)
+        gram_out[j, :, :rows] = lax.dot_general(
             expo, expo, NT, preferred_element_type=jnp.float32
         )
+        pl.when(keeps[j] != me)(gram_copy(j).start)
 
     cut = capacity // 2
     spans = (slice(cut, capacity + LANES), slice(0, cut))
@@ -323,16 +326,12 @@
         e_out[j, :, capacity:] = tail_of(top)
         for q in range(2):
             cross(j, q).start()
-        fill_gram(j, expo, top)
-        gram_copy(j, gives[j]).start()
 
     def keep(j):
         expo, top = produce(keeps[j])
         expo = expo.astype(jnp.bfloat16)
         pair[j, :, :capacity] = expo
         pair[j, :, capacity:] = tail_of(top)
-        fill_gram(half + j, expo, top)
-        pl.when(keeps[j] != me)(gram_copy(half + j, keeps[j]).start)
 
     def join(j, q):
         cross(j, q).wait_recv()
@@ -343,6 +342,9 @@
         def _():
             put(z_out.at[near, j], q, mixed)
             stream(near, j, q).start()
+
+        if q == 1:
+            fill_gram(j)
 
     def pass_near(j, q):
 
@@ -404,7 +406,7 @@
         came(chunks.at[pl.ds(0, groups - 1)], recv_chunk)
 
         def wait_grams():
-            came(gram_in.at[pl.ds(0, groups - 1)], recv_gram)
+            came(gram_in.at[pl.ds(0, outers - 1)], recv_gram)
 
         only(me < fits, wait_grams)
 
@@ -418,13 +420,13 @@
         def across_lanes(column):
             return jnp.sum(jnp.where(diagonal, column, 0.0), axis=0, keepdims=True)
 
-        gram_in[me] = gram_out[half + jnp.minimum(outer, half - 1)]
-        tops = [gram_in[source, :, middle : middle + 1] for source in range(groups)]
+        gram_in[outer] = gram_out[jnp.minimum(outer, half - 1)]
+        tops = [gram_in[source, :, middle : middle + 1] for source in range(outers)]
         top = tops[0]
         for other in tops[1:]:
             top = jnp.maximum(top, other)
         gram, total = 0.0, 0.0
-        for source in range(groups):
+        for source in range(outers):
             factor = jnp.exp2(tops[source] - top)
             total = total + factor * gram_in[source, :, rows : rows + 1]
             gram = gram + gram_in[source] * factor * across_lanes(factor)
@@ -467,15 +469,15 @@
 
             only(me < fits, whole)
 
-    agenda = [(1.54, attend, ()), (4.65, merge_targets, ())]
-    agenda += [(10.23, solve_first, ()), (10.7, solve_last, ())]
+    agenda = [(1.37, attend, ()), (7.21, merge_targets, ())]
+    agenda += [(15.23, solve_first, ()), (16.17, solve_last, ())]
     for j in range(half):
-        agenda += [(1.62 * j, give, (j,)), (3.0 + 1.22 * j, keep, (j,))]
+        agenda += [(1.39 * j, give, (j,)), (3.86 + 1.87 * j, keep, (j,))]
         for q in range(2):
-            at = 3.42 + 1.17 * j + 0.4 * q
+            at = 3.92 + 1.95 * j + 0.65 * q
             agenda.append((at, join, (j, q)))
-            agenda.append((at + 2.16, pass_near, (j, q)))
-            agenda.append((at + 4.75, pass_far, (j, q)))
+            agenda.append((at + 3.56, pass_near, (j, q)))
+            agenda.append((at + 6.84, pass_far, (j, q)))
     for _, act, at in sorted(agenda, key=lambda entry: entry[0]):
         act(*at)
     sent(table.at[pl.ds(0, heads * groups - 1)], send_q)
@@ -483,19 +485,19 @@
     sent(chunks.at[pl.ds(0, groups - 1)], send_chunk)
     sent(e_out, send_e)
     if groups == fits:
-        sent(gram_out.at[pl.ds(0, fits - 1)], send_gram)
+        sent(gram_out.at[pl.ds(0, half - 1)], send_gram)
     else:
-        pl.when(me < fits)(lambda: sent(gram_out.at[pl.ds(0, fits - 1)], send_gram))
+        pl.when(me < fits)(lambda: sent(gram_out.at[pl.ds(0, half - 1)], send_gram))
         pl.when(me >= fits)(lambda: sent(gram_out, send_gram))
     sent(z_out.at[near], send_z.at[near])
     pl.when(inside_line)(lambda: sent(z_out.at[far], send_z.at[far]))
     sent(p_all.at[pl.ds(0, half)], send_p)
     if groups == fits:
         came(x_all.at[pl.ds(0, fits - 1)], recv_x)
-        sent(gram_in.at[pl.ds(0, groups - 1), :, :width], send_x)
+        sent(x_all.at[pl.ds(0, groups - 1)], send_x)
     else:
         pl.when(me < fits)(lambda: came(x_all.at[pl.ds(0, fits - 1)], recv_x))
-        pl.when(me < fits)(lambda: sent(gram_in.at[pl.ds(0, groups - 1), :, :width], send_x))
+        pl.when(me < fits)(lambda: [copy.wait_send() for copy in results] and None)
         pl.when(me >= fits)(lambda: came(x_all, recv_x))
     came(p_all.at[pl.ds(0, half)], recv_p)
     count = jnp.int32(0)
@@ -541,7 +543,7 @@
     fits, capacity = indices.shape[1:]
     dma = pltpu.SemaphoreType.DMA
     params = dict(vmem_limit_bytes=(24 + rows // 8) * 1024 * 1024)
-    half = fits // PAIR
+    outers, half = groups // PAIR, fits // PAIR
     chunk = layers * rows // groups
     wide = (rows // LANES + 1) * LANES
     packed = (rows, capacity + LANES)
@@ -571,8 +573,8 @@
             pltpu.VMEM((groups, 2, chunk, width), jnp.float32),
             pltpu.VMEM((chunk, width), jnp.float32),
             pltpu.VMEM((groups, chunk, width), jnp.float32),
-            pltpu.VMEM((fits, rows, wide), jnp.float32),
-            pltpu.VMEM((groups, rows, wide), jnp.float32),
+            pltpu.VMEM((half, rows, wide), jnp.float32),
+            pltpu.VMEM((outers, rows, wide), jnp.float32),
             pltpu.VMEM((half,) + packed, jnp.bfloat16),
             pltpu.VMEM((half,) + packed, jnp.bfloat16),
             pltpu.VMEM((half,) + packed, jnp.bfloat16),

time: 38.2 us -> 37.2 us (0.974)
  Pallas kernels: 38 us -> 37 us
    pallas_call x1, Pallas kernels: 36.8 us -> 35.8 us  [on_device(): pl.pallas_call(fit_kernel, out_shape=(jax.ShapeDtypeStruct((SLOTS, rows,...]
where the time goes in v4:
time: 37.2 us; the launch traced here: 37 us
  Pallas kernels  37 us (99%)
    pallas_call x1, Pallas kernels, on_device(): pl.pallas_call(fit_kernel, out_shape=(jax.ShapeDtypeStruct((SLOTS, rows,...  35.8 us
    pallas_call x1, Pallas kernels, on_device(): pl.pallas_call(place_kernel, out_shape=jax.ShapeDtypeStruct((1, SLOTS, ca...  1.22 us

profile of v4, /device:TPU:0, one launch (start us, length us, event | category | flops | bytes accessed | tf_op | source)
XLA Modules:
  0.0 37.0 jit_solution(10981675429143574338)
XLA Ops:
  0.0 35.8 %shard_map.64 = (bf16[3,32,1024]{2,1,0:T(8,128)(2,1)S(1)}, f32[3,32,128]{2,1,0:T(8,128)S(1)}) custom-call(s32[1,8]{1,0:T(1,128)} %sizes_hbm.1, s32[1,8]{1,0:T(1,128)} %owners_hbm.1, bf16[8,128]{1,0:T(8,128)(2,1)} %bitcast.7, bf16[2,2048,128]{2,1,0:T(8,128)(2,1)} %bitcast.4, bf16[2,2048,128]{2,1,0:T(8,128)(2,1)} %bitcast.5, s32[8,1024]{1,0:T(8,128)} %bitcast.6), custom_call_target="tpu_custom_call" | custom-call | tf_op jit(solution)/shard_map/pallas_call | solution.py:550
  35.8 1.2 %shard_map.65 = bf16[1,3,1024,128]{3,2,1,0:T(8,128)(2,1)} custom-call(bf16[3,32,1024]{2,1,0:T(8,128)(2,1)S(1)} %get-tuple-element.7.p_ref, f32[3,32,128]{2,1,0:T(8,128)S(1)} %get-tuple-element.8.x_ref), custom_call_target="tpu_custom_call" | custom-call | tf_op jit(solution)/shard_map/pallas_call | solution.py:619
